TPU v7x, 32 devices: a whole 2x2x4 slice. The times are simulated.
32 devices in a mesh: grp: 2 (over y), seq: 16 (over z, x, core).
Axes of the slice: x: 2, y: 2, z: 4, core: 2. Of those that a mesh axis runs over, the one named last changes fastest.
Arguments:
- queries: bfloat16 [4096, 12288], P(('grp', 'seq')), parts along dimension 0, may hold values from -8 to 8
- sum_keys: bfloat16 [256, 768], P(('grp', 'seq')), parts along dimension 0, may hold values from -4 to 4
- sum_values: bfloat16 [256, 512], P(('grp', 'seq')), parts along dimension 0, may hold values from -24 to 24
- limits: int32 [64], P('grp'), parts along dimension 0, may hold values from 1 to 128, as said below
- valid_tokens: int32 [2], P('grp'), parts along dimension 0, may hold values from 1024 to 2048
Outputs:
- attended: bfloat16 [4096, 8192], P(('grp', 'seq')), parts along dimension 0
There are 2 independent parts, one for each index of `grp`. A program takes and returns all parts, laid end to end along the dimension named above; each array names one. Nothing has to cross between parts.
Inputs may be any that keep to these rules, and one draw needn't show every extreme that they name: limits[b] is at least 1 and at most max(1, (64 * b - 32) // 16 + 1), the number of summaries that end at or before the block's first token; the last block reaches this bound.
All inputs are finite; a program needn't handle non-finite values.
Results may differ from a plain program's by a relative error of at most 0.0027.
Values may be sent and summed in bfloat16 or wider, within the bound.
A program may use at most 64 MiB of HBM per device.

v0:
```python
import jax
import jax.numpy as jnp
from jax import lax
from jax.sharding import PartitionSpec as P

H = 64
G = 4
DK = 192
DV = 128
STRIDE = 16
CBLOCK = 32
QB = 64


def per_device(queries, sum_keys, sum_values, limits, valid_tokens):
    tok_rows = queries.shape[0]
    per_group = H // G
    inv_root = float(DK) ** (-0.5)
    usable = jnp.maximum((valid_tokens[0] - CBLOCK) // STRIDE + 1, 1)
    my_index = lax.axis_index("seq")
    block_count = tok_rows // QB
    local_blocks = jnp.arange(block_count, dtype=jnp.int32)
    block_ids = my_index * block_count + local_blocks
    table_ids = jnp.arange(limits.shape[0], dtype=jnp.int32)
    block_limits = jnp.sum(
        jnp.where(table_ids[None, :] == block_ids[:, None], limits[None, :], 0), axis=1
    )
    row_caps = jnp.repeat(jnp.minimum(block_limits, usable), QB)
    highest = jnp.max(row_caps)
    grouped = queries.reshape(tok_rows, G, per_group, DK)
    all_keys, all_values = (
        lax.all_gather(sum_keys, "seq", axis=0, tiled=True),
        lax.all_gather(sum_values, "seq", axis=0, tiled=True),
    )
    total = all_keys.shape[0]
    step_len = min(512, total)
    step_count = total // step_len

    def fold_block(block_pos, state_now):
        first_id = block_pos * step_len

        def update(current):
            run_max, run_sum, run_out = current
            key_block = lax.dynamic_slice_in_dim(all_keys, first_id, step_len, 0).reshape(
                step_len, G, DK
            )
            value_block = lax.dynamic_slice_in_dim(all_values, first_id, step_len, 0).reshape(
                step_len, G, DV
            )
            scores = (
                jnp.einsum("tgjd,sgd->tgjs", grouped, key_block, preferred_element_type=jnp.float32)
                * inv_root
            )
            summary_ids = first_id + jnp.arange(step_len, dtype=jnp.int32)
            visible = (summary_ids[None, :] < row_caps[:, None])[:, None, None, :]
            scores = jnp.where(visible, scores, -1e30)
            new_max = jnp.maximum(run_max, jnp.max(scores, axis=-1))
            rescale = jnp.exp(run_max - new_max)
            weights = jnp.where(visible, jnp.exp(scores - new_max[..., None]), 0.0)
            new_sum = run_sum * rescale + jnp.sum(weights, axis=-1)
            added = jnp.einsum(
                "tgjs,sgd->tgjd",
                weights.astype(jnp.bfloat16),
                value_block,
                preferred_element_type=jnp.float32,
            )
            return (new_max, new_sum, run_out * rescale[..., None] + added)

        def unchanged(current):
            return current

        return lax.cond(first_id < highest, update, unchanged, state_now)

    start_state = (
        jnp.full((tok_rows, G, per_group), -1e30, jnp.float32),
        jnp.zeros((tok_rows, G, per_group), jnp.float32),
        jnp.zeros((tok_rows, G, per_group, DV), jnp.float32),
    )
    run_max, run_sum, run_out = lax.fori_loop(0, step_count, fold_block, start_state)
    attended = (run_out / run_sum[..., None]).reshape(tok_rows, H * DV).astype(jnp.bfloat16)
    return attended


def solution(mesh):
    placed = (
        P(("grp", "seq"), None),
        P(("grp", "seq"), None),
        P(("grp", "seq"), None),
        P("grp"),
        P("grp"),
    )
    return jax.shard_map(
        per_device, mesh=mesh, in_specs=placed, out_specs=P(("grp", "seq"), None), check_vma=False
    )
```

profile of v0, /device:TPU:0, one launch (start us, length us, event | category | flops | bytes accessed | tf_op | source)
XLA Modules:
  0.0 68.0 jit_solution(9087807829274325061)
XLA Ops:
  0.7 0.8 %fusion.13 = s32[2]{0:T(128)S(1)} fusion(s32[32]{0:T(128)} %param.10, s32[2]{0:T(128)S(1)} %iota_add_fusion), kind=kLoop, calls=%fused_computation.22 | loop fusion | flops 190 | bytes 144 | tf_op jit(solution)/shard_map/reduce_sum | solution.py:25
  1.5 0.7 %broadcast_reduce_fusion = s32[]{:T(128)} fusion(s32[2]{0:T(128)S(1)} %broadcast_minimum_fusion), kind=kLoop, calls=%fused_computation.24 | loop fusion | flops 127 | bytes 12 | tf_op jit(solution)/shard_map/reduce_max | solution.py:29
  2.9 0.1 broadcast_in_dim.62
  3.0 23.7 %all_gather.7 = bf16[128,512]{1,0:T(8,128)(2,1)S(1)} all-gather(bf16[8,512]{1,0:T(8,128)(2,1)} %param.9), channel_id=1, replica_groups=mesh['grp'=2,'seq'=16] {'seq'}, dimensions={0}, use_global_device_ids=true | all-gather | bytes 139264 | tf_op jit(solution)/shard_map/all_gather | solution.py:33
  26.6 18.2 %all_gather.6 = bf16[128,768]{1,0:T(8,128)(2,1)S(1)} all-gather(bf16[8,768]{1,0:T(8,128)(2,1)} %param.8), channel_id=1, replica_groups=mesh['grp'=2,'seq'=16] {'seq'}, dimensions={0}, use_global_device_ids=true | all-gather | bytes 208896 | tf_op jit(solution)/shard_map/all_gather | solution.py:32
  44.8 0.6 broadcast_in_dim.63
  45.4 2.4 %broadcast_in_dim.64 = f32[128,4,16,128]{3,0,2,1:T(8,128)} broadcast(f32[]{:T(128)} %constant.59.clone.1), dimensions={} | broadcast | bytes 4194308 | tf_op jit(solution)/shard_map/broadcast_in_dim | solution.py:77
  47.9 12.8 %conditional.1 = ((f32[128,4,16]{0,2,1:T(8,128)}, f32[128,4,16,128]{3,0,2,1:T(8,128)})) conditional(s32[]{:T(128)} %convert_element_type.15, (f32[128,4,16]{0,2,1:T(8,128)}, f32[128,4,16,128]{3,0,2,1:T(8,128)}) %tuple.22, (s32[2,64]{1,0:T(2,128)S(1)}, bf16[128,768]{1,0:T(8,128)(2,1)S(1)}, bf16[128,12288]{1,0:T(8,128)(2,1)}, f32[128,4,16]{0,2,1:T(8,128)}, ...), branch_computations={%region_2.3_spmd, %region_3.0_spmd} | conditional | flops 686858240 | bytes 65930860 | solution.py:72
  47.9 0.7 %reshape.61 = bf16[128,4,128]{2,1,0:T(4,128)(2,1)} reshape(bf16[128,512]{1,0:T(8,128)(2,1)S(1)} %get-tuple-element.91) | data formatting | bytes 262144 | tf_op jit(solution)/shard_map/while/body/eval_jaxpr/cond/branch_1_fun/reshape | solution.py:47
  48.6 0.1 lt.24
  48.7 0.2 copy.19
  48.8 3.5 %copy.20 = bf16[128,12288]{0,1:T(8,128)(2,1)S(1)} copy(bf16[128,12288]{1,0:T(8,128)(2,1)} %get-tuple-element.112) | data formatting | bytes 6291456 | tf_op jit(solution)/shard_map
  52.3 0.9 %fusion = (f32[128,4,16]{0,2,1:T(8,128)S(1)}, f32[4,128,128,16]{2,1,3,0:T(8,128)S(1)}) fusion(pred[128,128]{0,1:T(8,128)(4,1)S(1)} %iota_compare_fusion, bf16[128,4,192,1]{0,2,3,1:T(8,128)(2,1)S(1)} %bitcast.30, bf16[128,4,16,192]{0,3,2,1:T(8,128)(2,1)S(1)} %bitcast.28), kind=kOutput, calls=%fused_computation.3 | convolution fusion | flops 405790720 | bytes 7585792 | tf_op jit(solution)/shard_map/while/body/eval_jaxpr/cond/branch_1_fun/tgjd,sgd->tgjs/dot_general | solution.py:51
  53.2 0.0 copy-start
  53.2 0.0 copy-start.2
  53.3 1.2 %fusion.2 = f32[128,4,16]{0,2,1:T(8,128)S(1)} fusion(f32[4,128,128,16]{2,1,3,0:T(8,128)S(1)} %get-tuple-element.119, f32[128,4,16]{0,2,1:T(8,128)S(1)} %broadcast_maximum_fusion, pred[128,128]{0,1:T(8,128)(4,1)S(1)} %iota_compare_fusion), kind=kLoop, calls=%fused_computation.5 | loop fusion | flops 5234688 | bytes 4276224 | tf_op jit(solution)/shard_map/while/body/eval_jaxpr/cond/branch_1_fun/reduce_sum | solution.py:60
  54.5 1.4 %subtract_exponential_fusion = (f32[128,4,16]{0,2,1:T(8,128)S(1)}, f32[128,4,16]{0,2,1:T(8,128)}) fusion(f32[128,4,16]{0,2,1:T(8,128)S(1)} %get-tuple-element.118, f32[128,4,16]{0,2,1:T(8,128)S(1)} %fusion.2, f32[128,4,16]{0,2,1:T(8,128)} %get-tuple-element.86), kind=kLoop, calls=%fused_computation.14 | loop fusion | flops 32768 | bytes 163840 | tf_op jit(solution)/shard_map/while/body/eval_jaxpr/cond/branch_1_fun/exp | solution.py:58
  55.9 0.0 copy-done
  55.9 0.0 copy-done.2
  55.9 2.8 %bitcast_add_fusion = f32[128,4,16,128]{3,0,2,1:T(8,128)S(1)} fusion(f32[128,4,16,128]{3,0,2,1:T(8,128)S(1)} %copy-done, f32[4,128,128,16]{2,1,3,0:T(8,128)S(1)} %get-tuple-element.119, f32[128,4,16]{0,2,1:T(8,128)S(1)} %get-tuple-element.116, f32[128,4,16]{0,2,1:T(8,128)S(1)} %broadcast_maximum_fusion, pred[128,128]{0,1:T(8,128)(4,1)S(1)} %iota_compare_fusion, ...), kind=kOutput, calls=%fused_computation | convolution fusion | flops 275775488 | bytes 12795904 | tf_op jit(solution)/shard_map/while/body/eval_jaxpr/cond/branch_1_fun/tgjs,sgd->tgjd/dot_general | solution.py:61
  58.7 0.0 copy-start.1
  58.7 1.9 %copy-done.1 = f32[128,4,16,128]{3,0,2,1:T(8,128)} copy-done((f32[128,4,16,128]{3,0,2,1:T(8,128)}, f32[128,4,16,128]{3,0,2,1:T(8,128)S(1)}, u32[]{:S(2)}) %copy-start.1) | copy-done | bytes 4194328 | tf_op jit(solution)/shard_map/while/body/eval_jaxpr/cond
  60.6 2.9 %divide_convert_fusion = bf16[128,4,16,128]{3,0,2,1:T(8,128)(2,1)S(1)} fusion(f32[128,4,16,128]{3,0,2,1:T(8,128)} %get-tuple-element.94, f32[128,4,16]{0,2,1:T(8,128)} %get-tuple-element.95), kind=kLoop, calls=%fused_computation.19 | loop fusion | flops 2097152 | bytes 6324224 | tf_op jit(solution)/shard_map/convert_element_type | solution.py:80
  63.5 1.4 %copy.21 = bf16[128,4,16,128]{3,2,1,0:T(8,128)(2,1)S(1)} copy(bf16[128,4,16,128]{3,0,2,1:T(8,128)(2,1)S(1)} %divide_convert_fusion) | data formatting | bytes 4194304 | tf_op jit(solution)/shard_map/convert_element_type | solution.py:80
  64.9 3.1 %copy.31 = bf16[16,8,64,128]{3,1,2,0:T(8,128)(2,1)} copy(bf16[16,8,64,128]{3,2,1,0:T(8,128)(2,1)S(1)} %bitcast.29) | data formatting | bytes 4194304
  (4 shorter events, 0.0 us)
Async XLA Ops:
  53.2 2.7 %copy-start = (f32[128,4,16,128]{3,0,2,1:T(8,128)S(1)}, f32[128,4,16,128]{3,0,2,1:T(8,128)}, u32[]{:S(2)}) copy-start(f32[128,4,16,128]{3,0,2,1:T(8,128)} %get-tuple-element.90) | copy-start | bytes 12582916 | tf_op jit(solution)/shard_map/while/body/eval_jaxpr/cond
  53.2 2.7 %copy-start.2 = (bf16[128,4,128]{2,1,0:T(4,128)(2,1)S(1)}, bf16[128,4,128]{2,1,0:T(4,128)(2,1)}, u32[]{:S(2)}) copy-start(bf16[128,4,128]{2,1,0:T(4,128)(2,1)} %reshape.61) | copy-start | bytes 393220 | tf_op jit(solution)/shard_map/while/body/eval_jaxpr/cond
  58.7 1.9 %copy-start.1 = (f32[128,4,16,128]{3,0,2,1:T(8,128)}, f32[128,4,16,128]{3,0,2,1:T(8,128)S(1)}, u32[]{:S(2)}) copy-start(f32[128,4,16,128]{3,0,2,1:T(8,128)S(1)} %bitcast_add_fusion) | copy-start | bytes 12582916 | tf_op jit(solution)/shard_map/while/body/eval_jaxpr/cond
where the time goes:
time: 68.2 us; the launch traced here: 68 us
  blocking collectives  41.9 us (61%)
  local copies, waits for them, and re-layouts  13.9 us (20%)
  other arithmetic  7.09 us (10%)
  matrix products  3.69 us (5%)
  between operations  1.36 us (2%)
    all_gather x1, blocking collectives, per_device(): lax.all_gather(sum_values, 'seq', axis=0, tiled=True)  23.7 us
    all_gather x1, blocking collectives, per_device(): lax.all_gather(sum_keys, 'seq', axis=0, tiled=True)  18.2 us
    another operation x2, local copies, waits for them, and re-layouts  3.64 us
    unnamed x1, local copies, waits for them, and re-layouts  3.12 us
    convert_element_type x1, other arithmetic, per_device(): (run_out / run_sum[..., None]).reshape(tok_rows, H * DV)  2.88 us
    dot_general x1, matrix products, update(): jnp.einsum('tgjs,sgd->tgjd', weights.astype(jnp.bfloat16), value_block, p...  2.79 us
    broadcast_in_dim x1, local copies, waits for them, and re-layouts, per_device(): jnp.zeros((tok_rows, G, per_group, DV), jnp.float32)  2.44 us
    cond x6, local copies, waits for them, and re-layouts  1.93 us

commit v1 on v0

--- a/solution.py
+++ b/solution.py
@@ -29,7 +29,9 @@
     highest = jnp.max(row_caps)
     grouped = queries.reshape(tok_rows, G, per_group, DK)
     all_keys, all_values = (
-        lax.all_gather(sum_keys, "seq", axis=0, tiled=True),
+        jnp.concatenate(
+            lax.all_to_all(jnp.stack([sum_keys] * lax.axis_size("seq")), "seq", 0, 0), axis=0
+        ),
         lax.all_gather(sum_values, "seq", axis=0, tiled=True),
     )
     total = all_keys.shape[0]

time: 68.2 us -> 56.8 us (0.83)
  blocking collectives: 41.9 us -> 22.1 us
  starting transfers between devices: 0 us -> 7.39 us
  local copies, waits for them, and re-layouts: 13.9 us -> 14.8 us
    all_gather x1 -> x0, blocking collectives: 18.2 us -> none  [per_device(): lax.all_gather(sum_keys, 'seq', axis=0, tiled=True)]
    all_to_all x0 -> x1, starting transfers between devices: none -> 7.39 us  [per_device(): lax.all_to_all(jnp.stack([sum_keys] * lax.axis_size('seq')), 'seq', 0, 0)]
    all_gather x1, blocking collectives: 23.7 us -> 22.1 us  [per_device(): lax.all_gather(sum_values, 'seq', axis=0, tiled=True)]
    another operation x2, local copies, waits for them, and re-layouts: 3.64 us -> 4.89 us
    cond x6 -> x4, local copies, waits for them, and re-layouts: 1.93 us -> 1.92 us
    unnamed x1 -> x3, local copies, waits for them, and re-layouts: 3.12 us -> 3.12 us
  transfers between devices with their start and end apart: 0 -> 1, of which waited for: 0 -> 0; matrix products, arithmetic and copies ran while one was open for 0% -> 8% of each run, Pallas kernels for 0% -> 0%
where the time goes in v1:
time: 56.8 us; the launch traced here: 56.4 us
  blocking collectives  22.1 us (39%)
  local copies, waits for them, and re-layouts  14.8 us (26%)
  starting transfers between devices  7.39 us (13%)
  other arithmetic  7.14 us (13%)
  matrix products  3.63 us (6%)
  between operations  1.41 us (2%)
    all_gather x1, blocking collectives, per_device(): lax.all_gather(sum_values, 'seq', axis=0, tiled=True)  22.1 us
    all_to_all x1, starting transfers between devices, per_device(): lax.all_to_all(jnp.stack([sum_keys] * lax.axis_size('seq')), 'seq', 0, 0)  7.39 us
    another operation x1, local copies, waits for them, and re-layouts  3.48 us
    unnamed x3, local copies, waits for them, and re-layouts  3.12 us
    convert_element_type x1, other arithmetic, per_device(): (run_out / run_sum[..., None]).reshape(tok_rows, H * DV)  2.88 us
    dot_general x1, matrix products, update(): jnp.einsum('tgjs,sgd->tgjd', weights.astype(jnp.bfloat16), value_block, p...  2.79 us
    broadcast_in_dim x1, local copies, waits for them, and re-layouts, per_device(): jnp.zeros((tok_rows, G, per_group, DV), jnp.float32)  2.44 us
    cond x4, local copies, waits for them, and re-layouts  1.92 us
  transfers between devices with their start and end apart: 1, of which 0 were waited for; matrix products, arithmetic and copies ran while one was open for 8% of the time, Pallas kernels for 0%

profile of v1, /device:TPU:0, one launch (start us, length us, event | category | flops | bytes accessed | tf_op | source)
XLA Modules:
  0.0 56.4 jit_solution(13903077542227281940)
XLA Ops:
  0.0 0.0 copy-start.2
  0.0 1.4 %stack.2 = bf16[16,8,768]{2,1,0:T(8,128)(2,1)} broadcast(bf16[8,768]{1,0:T(8,128)(2,1)} %param.8), dimensions={1,2} | broadcast | bytes 208896 | tf_op jit(solution)/shard_map/stack | solution.py:33
  1.4 7.4 %all-to-all-start = ((bf16[16,8,768]{2,1,0:T(8,128)(2,1)}), bf16[16,8,768]{2,1,0:T(8,128)(2,1)S(1)}, u32[]{:S(2)}, u32[]{:S(2)}) async-start(bf16[16,8,768]{2,1,0:T(8,128)(2,1)} %stack.2), calls=%async_computation | async-start | bytes 393216 | tf_op jit(solution)/shard_map/all_to_all | solution.py:33
  9.5 0.8 %fusion.15 = s32[2]{0:T(128)S(1)} fusion(s32[32]{0:T(128)} %param.10, s32[2]{0:T(128)S(1)} %iota_add_fusion), kind=kLoop, calls=%fused_computation.24 | loop fusion | flops 190 | bytes 144 | tf_op jit(solution)/shard_map/reduce_sum | solution.py:25
  10.3 0.8 %broadcast_reduce_fusion = s32[]{:T(128)} fusion(s32[2]{0:T(128)S(1)} %broadcast_minimum_fusion), kind=kLoop, calls=%fused_computation.26 | loop fusion | flops 127 | bytes 12 | tf_op jit(solution)/shard_map/reduce_max | solution.py:29
  11.8 0.6 %broadcast_in_dim.63 = f32[128,4,16]{0,2,1:T(8,128)} broadcast(f32[]{:T(128)} %constant.59.clone.1), dimensions={} | broadcast | bytes 32772 | tf_op jit(solution)/shard_map/broadcast_in_dim | solution.py:78
  12.4 2.4 %broadcast_in_dim.64 = f32[128,4,16,128]{3,0,2,1:T(8,128)} broadcast(f32[]{:T(128)} %constant.59.clone.1), dimensions={} | broadcast | bytes 4194308 | tf_op jit(solution)/shard_map/broadcast_in_dim | solution.py:79
  14.9 0.0 copy-done.2
  14.9 22.1 %all_gather.3 = bf16[128,512]{1,0:T(8,128)(2,1)S(1)} all-gather(bf16[8,512]{1,0:T(8,128)(2,1)S(1)} %copy-done.2), channel_id=1, replica_groups=mesh['grp'=2,'seq'=16] {'seq'}, dimensions={0}, use_global_device_ids=true | all-gather | bytes 139264 | tf_op jit(solution)/shard_map/all_gather | solution.py:35
  36.9 0.0 all-to-all-done
  36.9 0.1 broadcast_in_dim.62
  37.0 12.1 %conditional.1 = ((f32[128,4,16]{0,2,1:T(8,128)}, f32[128,4,16,128]{3,0,2,1:T(8,128)})) conditional(s32[]{:T(128)} %convert_element_type.15, (f32[128,4,16]{0,2,1:T(8,128)}, f32[128,4,16,128]{3,0,2,1:T(8,128)}) %tuple.22, (s32[2,64]{1,0:T(2,128)S(1)}, bf16[16,8,768]{2,1,0:T(8,128)(2,1)S(1)}, bf16[128,12288]{1,0:T(8,128)(2,1)}, ...), branch_computations={%region_2.3_spmd, %region_3.0_spmd} | conditional | flops 686858240 | bytes 65406544 | solution.py:74
  37.0 0.1 lt.24
  37.1 0.2 reshape.66
  37.4 3.5 %copy.20 = bf16[128,12288]{0,1:T(8,128)(2,1)S(1)} copy(bf16[128,12288]{1,0:T(8,128)(2,1)} %get-tuple-element.113) | data formatting | bytes 6291456 | tf_op jit(solution)/shard_map
  40.9 0.8 %fusion = (f32[128,4,16]{0,2,1:T(8,128)S(1)}, f32[4,128,128,16]{2,1,3,0:T(8,128)S(1)}) fusion(pred[128,128]{0,1:T(8,128)(4,1)S(1)} %iota_compare_fusion, bf16[128,4,16,192]{0,3,2,1:T(8,128)(2,1)S(1)} %bitcast.23, bf16[128,4,192,1]{2,1,0,3:T(4,128)(2,1)S(1)} %bitcast.25), kind=kOutput, calls=%fused_computation.3 | convolution fusion | flops 405790720 | bytes 7585792 | tf_op jit(solution)/shard_map/while/body/eval_jaxpr/cond/branch_1_fun/tgjd,sgd->tgjs/dot_general | solution.py:53
  41.7 0.0 copy-start
  41.7 1.2 %fusion.2 = f32[128,4,16]{0,2,1:T(8,128)S(1)} fusion(f32[4,128,128,16]{2,1,3,0:T(8,128)S(1)} %get-tuple-element.120, f32[128,4,16]{0,2,1:T(8,128)S(1)} %broadcast_maximum_fusion, pred[128,128]{0,1:T(8,128)(4,1)S(1)} %iota_compare_fusion), kind=kLoop, calls=%fused_computation.5 | loop fusion | flops 5234688 | bytes 4276224 | tf_op jit(solution)/shard_map/while/body/eval_jaxpr/cond/branch_1_fun/reduce_sum | solution.py:62
  43.0 1.4 %subtract_exponential_fusion = (f32[128,4,16]{0,2,1:T(8,128)S(1)}, f32[128,4,16]{0,2,1:T(8,128)}) fusion(f32[128,4,16]{0,2,1:T(8,128)S(1)} %get-tuple-element.119, f32[128,4,16]{0,2,1:T(8,128)S(1)} %fusion.2, f32[128,4,16]{0,2,1:T(8,128)} %get-tuple-element.87), kind=kLoop, calls=%fused_computation.16 | loop fusion | flops 32768 | bytes 163840 | tf_op jit(solution)/shard_map/while/body/eval_jaxpr/cond/branch_1_fun/exp | solution.py:60
  44.4 0.0 copy-done
  44.4 2.8 %bitcast_add_fusion = f32[128,4,16,128]{3,0,2,1:T(8,128)S(1)} fusion(f32[128,4,16,128]{3,0,2,1:T(8,128)S(1)} %copy-done, f32[4,128,128,16]{2,1,3,0:T(8,128)S(1)} %get-tuple-element.120, f32[128,4,16]{0,2,1:T(8,128)S(1)} %get-tuple-element.117, f32[128,4,16]{0,2,1:T(8,128)S(1)} %broadcast_maximum_fusion, pred[128,128]{0,1:T(8,128)(4,1)S(1)} %iota_compare_fusion, ...), kind=kOutput, calls=%fused_computation | convolution fusion | flops 275775488 | bytes 12795904 | tf_op jit(solution)/shard_map/while/body/eval_jaxpr/cond/branch_1_fun/tgjs,sgd->tgjd/dot_general | solution.py:63
  47.2 0.0 copy-start.1
  47.2 1.9 %copy-done.1 = f32[128,4,16,128]{3,0,2,1:T(8,128)} copy-done((f32[128,4,16,128]{3,0,2,1:T(8,128)}, f32[128,4,16,128]{3,0,2,1:T(8,128)S(1)}, u32[]{:S(2)}) %copy-start.1) | copy-done | bytes 4194328 | tf_op jit(solution)/shard_map/while/body/eval_jaxpr/cond
  49.1 2.9 %divide_convert_fusion = bf16[128,4,16,128]{3,0,2,1:T(8,128)(2,1)S(1)} fusion(f32[128,4,16,128]{3,0,2,1:T(8,128)} %get-tuple-element.95, f32[128,4,16]{0,2,1:T(8,128)} %get-tuple-element.96), kind=kLoop, calls=%fused_computation.21 | loop fusion | flops 2097152 | bytes 6324224 | tf_op jit(solution)/shard_map/convert_element_type | solution.py:82
  52.0 1.4 %copy.21 = bf16[128,4,16,128]{3,2,1,0:T(8,128)(2,1)S(1)} copy(bf16[128,4,16,128]{3,0,2,1:T(8,128)(2,1)S(1)} %divide_convert_fusion) | data formatting | bytes 4194304 | tf_op jit(solution)/shard_map/convert_element_type | solution.py:82
  53.3 3.1 %copy.37 = bf16[16,8,64,128]{3,1,2,0:T(8,128)(2,1)} copy(bf16[16,8,64,128]{3,2,1,0:T(8,128)(2,1)S(1)} %bitcast.24) | data formatting | bytes 4194304
  (5 shorter events, 0.1 us)
Async XLA Ops:
  0.0 14.9 %copy-start.2 = (bf16[8,512]{1,0:T(8,128)(2,1)S(1)}, bf16[8,512]{1,0:T(8,128)(2,1)}, u32[]{:S(2)}) copy-start(bf16[8,512]{1,0:T(8,128)(2,1)} %param.9) | copy-start | bytes 24580
  1.4 35.5 %all-to-all-start = ((bf16[16,8,768]{2,1,0:T(8,128)(2,1)}), bf16[16,8,768]{2,1,0:T(8,128)(2,1)S(1)}, u32[]{:S(2)}, u32[]{:S(2)}) async-start(bf16[16,8,768]{2,1,0:T(8,128)(2,1)} %stack.2), calls=%async_computation | async-start | bytes 393216 | tf_op jit(solution)/shard_map/all_to_all | solution.py:33
  41.7 2.6 %copy-start = (f32[128,4,16,128]{3,0,2,1:T(8,128)S(1)}, f32[128,4,16,128]{3,0,2,1:T(8,128)}, u32[]{:S(2)}) copy-start(f32[128,4,16,128]{3,0,2,1:T(8,128)} %get-tuple-element.91) | copy-start | bytes 12582916 | tf_op jit(solution)/shard_map/while/body/eval_jaxpr/cond
  47.2 1.9 %copy-start.1 = (f32[128,4,16,128]{3,0,2,1:T(8,128)}, f32[128,4,16,128]{3,0,2,1:T(8,128)S(1)}, u32[]{:S(2)}) copy-start(f32[128,4,16,128]{3,0,2,1:T(8,128)S(1)} %bitcast_add_fusion) | copy-start | bytes 12582916 | tf_op jit(solution)/shard_map/while/body/eval_jaxpr/cond
